TPU v7x, 32 devices: a whole 2x2x4 slice. The times are simulated.
32 devices in a mesh: member: 2 (over x), mp: 16 (over z, y, core).
Axes of the slice: x: 2, y: 2, z: 4, core: 2. Of those that a mesh axis runs over, the one named last changes fastest.
Arguments:
- nodes: bfloat16 [2048, 4096], P(('member', 'mp')), parts along dimension 0, may hold values from -6 to 6
- norm_gain: float32 [4096], replicated, may hold values from 0.1 to 1.9
- w_in: bfloat16 [4096, 16384], P(None, 'mp'), may hold values from -0.09375 to 0.09375
- b_in: float32 [16384], P('mp'), may hold values from -3 to 3
- w_out: bfloat16 [16384, 4096], P('mp'), may hold values from -0.046875 to 0.046875
- b_out: float32 [4096], replicated, may hold values from -3 to 3
Outputs:
- updated: bfloat16 [2048, 4096], P(('member', 'mp')), parts along dimension 0
There are 2 independent parts, one for each index of `member`. A program takes and returns all parts, laid end to end along the dimension named above; an argument that names none is the same for every part. Nothing has to cross between parts.
All inputs are finite; a program needn't handle non-finite values.
Results may differ from a plain program's by a relative error of at most 0.015.
Values may be sent and summed in bfloat16 or wider, within the bound.
A program may use at most 128 MiB of HBM per device.

v0:
```python
import jax
import jax.numpy as jnp
from jax import lax
from jax.sharding import PartitionSpec as P


def normalize(rows, norm_gain):
    values = rows.astype(jnp.float32)
    mean = jnp.mean(values, axis=1, keepdims=True)
    var = jnp.mean((values - mean) ** 2, axis=1, keepdims=True)
    return ((values - mean) / jnp.sqrt(var + 1e-05) * norm_gain).astype(jnp.bfloat16)


def local(nodes, norm_gain, w_in, b_in, w_out, b_out):
    source = normalize(nodes, norm_gain)
    pre = (
        jnp.dot(
            lax.all_gather(source, "mp", axis=0, tiled=True),
            w_in,
            preferred_element_type=jnp.float32,
        )
        + b_in
    )
    gathered = jax.nn.gelu(pre, approximate=True).astype(jnp.bfloat16)
    summed = lax.psum_scatter(
        jnp.dot(gathered, w_out, preferred_element_type=jnp.float32).astype(jnp.bfloat16),
        "mp",
        scatter_dimension=0,
        tiled=True,
    ).astype(jnp.float32)
    return (nodes.astype(jnp.float32) + summed + b_out).astype(jnp.bfloat16)


def solution(mesh):
    return jax.shard_map(
        local,
        mesh=mesh,
        in_specs=(P(("member", "mp"), None), P(), P(None, "mp"), P("mp"), P("mp", None), P()),
        out_specs=P(("member", "mp"), None),
        check_vma=False,
    )
```

profile of v0, /device:TPU:9, one launch (start us, length us, event | category | flops | bytes accessed | tf_op | source)
XLA Modules:
  0.0 225.3 jit_solution(7028838983084275887)
XLA Ops:
  6.5 0.0 all-gather.2.cloned.1.call-start
  6.5 1.2 convert_reduce_fusion
  7.8 1.3 fusion.18
  9.1 2.1 fusion.20
  11.2 0.0 all-gather.2.cloned.1.call-update
  11.2 0.0 reduce-scatter.2.cloned.1.call-start
  11.3 75.7 %all-gather.2.cloned.1.call-done = bf16[1024,4096]{1,0:T(8,128)(2,1)} async-done(((bf16[64,4096]{1,0:T(8,128)(2,1)}), bf16[1024,4096]{1,0:T(8,128)(2,1)}) %all-gather.2.cloned.1.call-update) | async-done | bytes 8388624 | tf_op jit(solution)/shard_map/all_gather | solution.py:18
  87.0 27.6 %convolution_convert_fusion = bf16[1024,4096]{1,0:T(8,128)(2,1)} fusion(bf16[1024,4096]{1,0:T(8,128)(2,1)} %param.10, bf16[1024,4096]{1,0:T(8,128)(2,1)} %all-gather.2.cloned.1.call-done, bf16[4096,1024]{1,0:T(8,128)(2,1)} %param.8, f32[1024]{0:T(1024)} %param.9), kind=kOutput, calls=%fused_computation | convolution fusion | flops 17194549248 | bytes 33558528 | tf_op jit(solution)/shard_map/dot_general | solution.py:26
  114.6 0.0 copy-start
  114.6 0.0 copy-start.1
  114.6 0.0 reduce-scatter.2.cloned.1.call-update
  114.6 101.8 %reduce-scatter.2.cloned.1.call-done = bf16[64,4096]{1,0:T(8,128)(2,1)} async-done(((bf16[1024,4096]{1,0:T(8,128)(2,1)}), bf16[64,4096]{1,0:T(8,128)(2,1)}) %reduce-scatter.2.cloned.1.call-update) | async-done | bytes 524304 | tf_op jit(solution)/shard_map/reduce_scatter | solution.py:25
  216.5 0.0 copy-done
  216.5 0.0 copy-done.1
  216.5 2.0 fusion.22
  (2 shorter events, 0.0 us)
Async XLA Ops:
  6.5 80.5 %all-gather.2.cloned.1.call-start = ((), (), s32[]{:S(2)}) async-start(), calls=%async_computation.1 | async-start | bytes 8912896 | tf_op jit(solution)/shard_map/all_gather | solution.py:18
  11.2 205.2 %reduce-scatter.2.cloned.1.call-start = ((), (), s32[]{:S(2)}) async-start(), calls=%async_computation.2 | async-start | bytes 8912896 | tf_op jit(solution)/shard_map/reduce_scatter | solution.py:25
  114.6 101.9 %copy-start = (bf16[64,4096]{1,0:T(8,128)(2,1)S(1)}, bf16[64,4096]{1,0:T(8,128)(2,1)}, u32[]{:S(2)}) copy-start(bf16[64,4096]{1,0:T(8,128)(2,1)} %param.6) | copy-start | bytes 1572868
  114.6 101.9 %copy-start.1 = (f32[4096]{0:T(1024)S(1)}, f32[4096]{0:T(1024)}, u32[]{:S(2)}) copy-start(f32[4096]{0:T(1024)} %param.11) | copy-start | bytes 49156
Sparse Core Ops, SparseCore 0:
  11.3 75.6 all-gather.1
  114.7 101.6 reduce-scatter.1
where the time goes:
time: 227 us; the launch traced here: 225 us
  waiting for transfers between devices  178 us (78%)
  matrix products  27.6 us (12%)
  between operations  13.4 us (6%)
  other arithmetic  6.63 us (3%)
    reduce_scatter x1, waiting for transfers between devices, local(): lax.psum_scatter(jnp.dot(gathered, w_out, preferred_element_type=jnp.floa...  102 us
    all_gather x1, waiting for transfers between devices, local(): lax.all_gather(source, 'mp', axis=0, tiled=True)  75.7 us
    dot_general x1, matrix products, local(): jnp.dot(gathered, w_out, preferred_element_type=jnp.float32)  27.6 us
  transfers between devices with their start and end apart: 2, of which 2 were waited for; matrix products, arithmetic and copies ran while one was open for 0% of the time, Pallas kernels for 0%

commit v1 on v0

v1 whole, which is shorter than its diff:
```python
import functools

import jax
import jax.numpy as jnp
from jax import lax
from jax.experimental import pallas as pl
from jax.experimental.pallas import tpu as pltpu
from jax.sharding import PartitionSpec as P

MESH = pl.DeviceIdType.MESH
STRIP = 16
TILE = 256


def flip(value, bits):
    place = 1
    out = value
    while place <= bits:
        if bits & place:
            out = out + place - 2 * place * lax.rem(value // place, 2)
        place *= 2
    return out


def kernel(
    layers, nodes, gain, w_in_hbm, b_in, w_out_hbm, b_out, out,
    rows_all, w_in, w_out, hidden, part, from_core, from_y, from_z,
    w_sem, zs, zr, ys, yr, cs, cr, rcs, rcr, rys, ryr, rzs, rzr,
):
    m, d = nodes.shape
    f = w_in.shape[1]
    me = lax.axis_index("mp")
    a = me // 4
    b = lax.rem(me // 2, 2)
    c = lax.rem(me, 2)
    group = 4 * m

    def device(aa, bb, cc):
        return {"mp": aa * 4 + bb * 2 + cc}

    loads = [
        pltpu.make_async_copy(w_in_hbm, w_in, w_sem.at[0]),
        pltpu.make_async_copy(w_out_hbm, w_out, w_sem.at[1]),
    ]
    for load in loads:
        load.start()

    barrier = pltpu.get_barrier_semaphore()
    partners = [device(flip(a, j), b, c) for j in range(1, layers)]
    partners += [device(a, 1 - b, c), device(a, b, 1 - c)]
    for partner in partners:
        pl.semaphore_signal(barrier, inc=1, device_id=partner, device_id_type=MESH)

    def block(ref, aa, bb, cc):
        start = aa * group + (bb * 2 + cc) * m
        return ref.at[pl.ds(pl.multiple_of(start, m), m), :]

    mine = a * group + (b * 2 + c) * m

    def norm_strip(i, carry):
        at = pl.multiple_of(i * STRIP, STRIP)
        values = nodes[pl.ds(at, STRIP), :].astype(jnp.float32)
        mean = jnp.mean(values, axis=1, keepdims=True)
        var = jnp.mean((values - mean) ** 2, axis=1, keepdims=True)
        normed = (values - mean) / jnp.sqrt(var + 1e-05) * gain[...]
        rows_all[pl.ds(pl.multiple_of(mine + at, STRIP), STRIP), :] = normed.astype(
            jnp.bfloat16
        )
        return carry

    lax.fori_loop(0, m // STRIP, norm_strip, 0)
    pl.semaphore_wait(barrier, len(partners))

    sent = []

    def remote(src, dst, send, recv, target):
        return pltpu.make_async_remote_copy(
            src_ref=src, dst_ref=dst, send_sem=send, recv_sem=recv,
            device_id=target, device_id_type=MESH,
        )

    def send(*args):
        copy = remote(*args)
        copy.start()
        sent.append(copy)

    def arrived(dst, send_sem, recv_sem):
        remote(dst, dst, send_sem, recv_sem, device(a, b, 1 - c)).wait_recv()

    def gather_z(j):
        g = flip(a, j)
        own = block(rows_all, g, b, c)
        if j:
            arrived(own, zs.at[j], zr.at[j])
        send(own, own, ys.at[j], yr.at[j], device(a, 1 - b, c))
        send(own, own, cs.at[2 * j], cr.at[2 * j], device(a, b, 1 - c))

    def gather_y(j):
        g = flip(a, j)
        other = block(rows_all, g, 1 - b, c)
        arrived(other, ys.at[j], yr.at[j])
        send(other, other, cs.at[2 * j + 1], cr.at[2 * j + 1], device(a, b, 1 - c))

    def gather_c(j):
        g = flip(a, j)
        arrived(block(rows_all, g, b, 1 - c), cs.at[2 * j], cr.at[2 * j])
        arrived(block(rows_all, g, 1 - b, 1 - c), cs.at[2 * j + 1], cr.at[2 * j + 1])

    def compute(j):
        g = flip(a, j)
        rows = pl.ds(pl.multiple_of(g * group, group), group)

        def first(i, carry):
            cols = pl.ds(pl.multiple_of(i * TILE, TILE), TILE)
            pre = jnp.dot(
                rows_all[rows, :], w_in[:, cols], preferred_element_type=jnp.float32
            )
            pre = pre + b_in[:, cols]
            hidden[:, cols] = jax.nn.gelu(pre, approximate=True).astype(jnp.bfloat16)
            return carry

        def second(i, carry):
            cols = pl.ds(pl.multiple_of(i * TILE, TILE), TILE)
            share = jnp.dot(
                hidden[...], w_out[:, cols], preferred_element_type=jnp.float32
            )
            part[rows, cols] = share.astype(jnp.bfloat16)
            return carry

        if j == 0:
            loads[0].wait()
        lax.fori_loop(0, f // TILE, first, 0)
        if j == 0:
            loads[1].wait()
        lax.fori_loop(0, d // TILE, second, 0)
        for bb in range(2):
            send(
                block(part, g, bb, 1 - c), from_core.at[2 * j + bb],
                rcs.at[2 * j + bb], rcr.at[2 * j + bb], device(a, b, 1 - c),
            )

    def add(g, bb, landed):
        start = g * group + (bb * 2 + c) * m

        def strip(i, carry):
            at = pl.multiple_of(i * STRIP, STRIP)
            here = pl.ds(pl.multiple_of(start + at, STRIP), STRIP)
            total = part[here, :].astype(jnp.float32) + landed[
                pl.ds(at, STRIP), :
            ].astype(jnp.float32)
            part[here, :] = total.astype(jnp.bfloat16)
            return carry

        lax.fori_loop(0, m // STRIP, strip, 0)

    def reduce_c(j):
        g = flip(a, j)
        for bb in range(2):
            arrived(from_core.at[2 * j + bb], rcs.at[2 * j + bb], rcr.at[2 * j + bb])
        add(g, 1 - b, from_core.at[2 * j + 1 - b])
        send(
            block(part, g, 1 - b, c), from_y.at[j], rys.at[j], ryr.at[j],
            device(a, 1 - b, c),
        )
        add(g, b, from_core.at[2 * j + b])

    def reduce_y(j):
        g = flip(a, j)
        arrived(from_y.at[j], rys.at[j], ryr.at[j])
        add(g, b, from_y.at[j])
        if j:
            send(
                block(part, g, b, c), from_z.at[j], rzs.at[j], rzr.at[j],
                device(g, b, c),
            )

    own = block(rows_all, a, b, c)
    for j in range(1, layers):
        send(own, own, zs.at[j], zr.at[j], device(flip(a, j), b, c))
    gather_z(0)
    gather_y(0)
    if layers > 1:
        gather_z(1)
    for j in range(layers):
        gather_c(j)
        compute(j)
        if j >= 1:
            reduce_y(j - 1)
        if j + 1 < layers:
            gather_y(j + 1)
        if j + 2 < layers:
            gather_z(j + 2)
        reduce_c(j)
    reduce_y(layers - 1)
    for j in range(1, layers):
        arrived(from_z.at[j], rzs.at[j], rzr.at[j])

    def final(i, carry):
        at = pl.multiple_of(i * STRIP, STRIP)
        here = pl.ds(at, STRIP)
        total = part[pl.ds(pl.multiple_of(mine + at, STRIP), STRIP), :].astype(jnp.float32)
        for j in range(1, layers):
            total = total + from_z[j, here, :].astype(jnp.float32)
        total = nodes[here, :].astype(jnp.float32) + total + b_out[...]
        out[here, :] = total.astype(jnp.bfloat16)
        return carry

    lax.fori_loop(0, m // STRIP, final, 0)
    for copy in sent:
        copy.wait_send()


def solution(mesh):
    n = mesh.shape["mp"]
    layers = n // 4

    def local(nodes, norm_gain, w_in, b_in, w_out, b_out):
        m, d = nodes.shape
        f = w_in.shape[1]
        bf = jnp.bfloat16
        vmem = pl.BlockSpec(memory_space=pltpu.VMEM)
        hbm = pl.BlockSpec(memory_space=pl.ANY)
        dma = pltpu.SemaphoreType.DMA
        flops = 4 * n * m * d * f
        return pl.pallas_call(
            functools.partial(kernel, layers),
            out_shape=jax.ShapeDtypeStruct((m, d), bf),
            in_specs=[vmem, vmem, hbm, vmem, hbm, vmem],
            out_specs=vmem,
            scratch_shapes=[
                pltpu.VMEM((n * m, d), bf),
                pltpu.VMEM((d, f), bf),
                pltpu.VMEM((f, d), bf),
                pltpu.VMEM((4 * m, f), bf),
                pltpu.VMEM((n * m, d), bf),
                pltpu.VMEM((2 * layers, m, d), bf),
                pltpu.VMEM((layers, m, d), bf),
                pltpu.VMEM((layers, m, d), bf),
                dma((2,)),
                dma((layers,)), dma((layers,)),
                dma((layers,)), dma((layers,)),
                dma((2 * layers,)), dma((2 * layers,)),
                dma((2 * layers,)), dma((2 * layers,)),
                dma((layers,)), dma((layers,)),
                dma((layers,)), dma((layers,)),
            ],
            compiler_params=pltpu.CompilerParams(
                collective_id=0, has_side_effects=True, vmem_limit_bytes=67043328
            ),
            cost_estimate=pl.CostEstimate(
                flops=flops, bytes_accessed=4 * d * f, transcendentals=n * m * f
            ),
            name="ffn",
        )(nodes, norm_gain[None], w_in, b_in[None], w_out, b_out[None])

    return jax.shard_map(
        local,
        mesh=mesh,
        in_specs=(P(("member", "mp"), None), P(), P(None, "mp"), P("mp"), P("mp", None), P()),
        out_specs=P(("member", "mp"), None),
        check_vma=False,
    )
```

time: 227 us -> 137 us (0.60)
  waiting for transfers between devices: 178 us -> 0 us
  Pallas kernels: 0 us -> 135 us
  matrix products: 27.6 us -> 0 us
  between operations: 13.4 us -> 0.01 us
  other arithmetic: 6.63 us -> 0 us
    pallas_call x0 -> x1, Pallas kernels: none -> 135 us  [local(): pl.pallas_call(functools.partial(kernel, layers), out_shape=jax.ShapeDtyp...]
    reduce_scatter x1 -> x0, waiting for transfers between devices: 102 us -> none  [local(): lax.psum_scatter(jnp.dot(gathered, w_out, preferred_element_type=jnp.floa...]
    all_gather x1 -> x0, waiting for transfers between devices: 75.7 us -> none  [local(): lax.all_gather(source, 'mp', axis=0, tiled=True)]
    dot_general x1 -> x0, matrix products: 27.6 us -> none  [local(): jnp.dot(gathered, w_out, preferred_element_type=jnp.float32)]
    convert_element_type x2 -> x0, other arithmetic: 4.07 us -> none  [the longest x1 2.08 us: normalize(): ((values - mean) / jnp.sqrt(var + 1e-05) * norm_gain).astype(jnp.bfloat16)]
    reduce_sum x2 -> x0, other arithmetic: 2.56 us -> none  [the longest x1 1.35 us: normalize(): var = jnp.mean((values - mean) ** 2, axis=1, keepdims=True)]
  transfers between devices with their start and end apart: 2 -> 0, of which waited for: 2 -> 0; matrix products, arithmetic and copies ran while one was open for 0% -> 0% of each run, Pallas kernels for 0% -> 0%
where the time goes in v1:
time: 137 us
  Pallas kernels  135 us (99%)
  local copies, waits for them, and re-layouts  1.87 us (1%)
    pallas_call x1, Pallas kernels, local(): pl.pallas_call(functools.partial(kernel, layers), out_shape=jax.ShapeDtyp...  135 us

profile of v1, /device:TPU:9, one launch (start us, length us, event | category | flops | bytes accessed | tf_op | source)
XLA Modules:
  0.0 137.3 jit_solution(13604295172682782932)
XLA Ops:
  0.0 135.4 %ffn.1 = bf16[64,4096]{1,0:T(8,128)(2,1)} custom-call(bf16[64,4096]{1,0:T(8,128)(2,1)} %nodes.1, f32[1,4096]{1,0:T(1,128)} %bitcast.3, bf16[4096,1024]{1,0:T(8,128)(2,1)} %w_in_hbm.1, f32[1,1024]{1,0:T(1,128)} %bitcast.5, bf16[1024,4096]{1,0:T(8,128)(2,1)} %w_out_hbm.1, f32[1,4096]{1,0:T(1,128)} %bitcast.4), custom_call_target="tpu_custom_call" | custom-call | flops 17179869184 | bytes 16777216 | tf_op jit(solution)/shard_map/ffn/pallas_call | solution.py:225
  135.4 1.9 %copy.8 = bf16[64,4096]{1,0:T(8,128)(2,1)} copy(bf16[64,4096]{1,0:T(8,128)(2,1)} %ffn.1) | data formatting | bytes 1048576

commit v2 on v1

--- a/solution.py
+++ b/solution.py
@@ -9,7 +9,8 @@
 
 MESH = pl.DeviceIdType.MESH
 STRIP = 16
-TILE = 256
+TILE = 512
+HALVES = 2
 
 
 def flip(value, bits):
@@ -25,7 +26,7 @@
 def kernel(
     layers, nodes, gain, w_in_hbm, b_in, w_out_hbm, b_out, out,
     rows_all, w_in, w_out, hidden, part, from_core, from_y, from_z,
-    w_sem, zs, zr, ys, yr, cs, cr, rcs, rcr, rys, ryr, rzs, rzr,
+    w_sem, zs, zr, qs, qr, ys, yr, cs, cr, rcs, rcr, rys, ryr, rzs, rzr,
 ):
     m, d = nodes.shape
     f = w_in.shape[1]
@@ -87,27 +88,90 @@
     def arrived(dst, send_sem, recv_sem):
         remote(dst, dst, send_sem, recv_sem, device(a, b, 1 - c)).wait_recv()
 
-    def gather_z(j):
-        g = flip(a, j)
+    early = m // 2
+    late = m - early
+
+    def xor(x, y):
+        total, place = 0, 1
+        while place < layers:
+            total = total + place * lax.rem(x // place + y // place, 2)
+            place *= 2
+        return total
+
+    mid = lax.rem((a + 1) // 2, 2) if layers == 4 else 0
+    slots = list(range(layers))
+    if layers == 4:
+        slots[2], slots[3] = 2 + mid, 3 - mid
+    groups = [xor(a, jj) for jj in slots]
+
+    def late_rows(ref, aa, bb, cc):
+        start = aa * group + (bb * 2 + cc) * m + early
+        return ref.at[pl.ds(pl.multiple_of(start, STRIP), late), :]
+
+    def early_rows(ref, aa, bb, cc):
+        start = aa * group + (bb * 2 + cc) * m
+        return ref.at[pl.ds(pl.multiple_of(start, STRIP), early), :]
+
+    guarded = []
+
+    def pass_on(p, rows, send_sems, recv_sems):
+        g = groups[p]
+        for step in (1, -1):
+            if p == 0:
+                sem = send_sems.at[0 if step == 1 else layers]
+                ready = a < layers - 1 if step == 1 else a > 0
+            else:
+                sem = send_sems.at[slots[p]]
+                ready = (
+                    jnp.logical_and(g < a, a < layers - 1)
+                    if step == 1
+                    else jnp.logical_and(g > a, a > 0)
+                )
+            to = lax.rem(a + step + layers, layers)
+            copy = remote(rows, rows, sem, recv_sems.at[xor(to, g)], device(to, b, c))
+
+            @pl.when(ready)
+            def _(copy=copy):
+                copy.start()
+
+            guarded.append((ready, copy))
+
+    def gather_z(p):
+        g, j = groups[p], slots[p]
         own = block(rows_all, g, b, c)
-        if j:
+        if p:
             arrived(own, zs.at[j], zr.at[j])
-        send(own, own, ys.at[j], yr.at[j], device(a, 1 - b, c))
+            pass_on(p, own, zs, zr)
+            first = early_rows(rows_all, g, b, c)
+        else:
+            pass_on(p, own, zs, zr)
+            first = own
+        send(first, first, ys.at[j], yr.at[j], device(a, 1 - b, c))
         send(own, own, cs.at[2 * j], cr.at[2 * j], device(a, b, 1 - c))
 
-    def gather_y(j):
-        g = flip(a, j)
+    def gather_q(p):
+        g, j = groups[p], slots[p]
+        rows = late_rows(rows_all, g, 1 - b, c)
+        if p:
+            arrived(rows, qs.at[j], qr.at[j])
+        pass_on(p, rows, qs, qr)
+
+    def gather_y(p):
+        g, j = groups[p], slots[p]
         other = block(rows_all, g, 1 - b, c)
-        arrived(other, ys.at[j], yr.at[j])
+        if p:
+            arrived(early_rows(rows_all, g, 1 - b, c), ys.at[j], yr.at[j])
+        else:
+            arrived(other, ys.at[j], yr.at[j])
         send(other, other, cs.at[2 * j + 1], cr.at[2 * j + 1], device(a, b, 1 - c))
 
-    def gather_c(j):
-        g = flip(a, j)
+    def gather_c(p):
+        g, j = groups[p], slots[p]
         arrived(block(rows_all, g, b, 1 - c), cs.at[2 * j], cr.at[2 * j])
         arrived(block(rows_all, g, 1 - b, 1 - c), cs.at[2 * j + 1], cr.at[2 * j + 1])
 
-    def compute(j):
-        g = flip(a, j)
+    def compute(p):
+        g, j = groups[p], slots[p]
         rows = pl.ds(pl.multiple_of(g * group, group), group)
 
         def first(i, carry):
@@ -127,10 +191,10 @@
             part[rows, cols] = share.astype(jnp.bfloat16)
             return carry
 
-        if j == 0:
+        if p == 0:
             loads[0].wait()
         lax.fori_loop(0, f // TILE, first, 0)
-        if j == 0:
+        if p == 0:
             loads[1].wait()
         lax.fori_loop(0, d // TILE, second, 0)
         for bb in range(2):
@@ -139,8 +203,14 @@
                 rcs.at[2 * j + bb], rcr.at[2 * j + bb], device(a, b, 1 - c),
             )
 
-    def add(g, bb, landed):
-        start = g * group + (bb * 2 + c) * m
+    half = m // HALVES
+
+    def piece(ref, aa, bb, cc, h):
+        start = aa * group + (bb * 2 + cc) * m + h * half
+        return ref.at[pl.ds(pl.multiple_of(start, half), half), :]
+
+    def add(g, bb, landed, skip, count):
+        start = g * group + (bb * 2 + c) * m + skip
 
         def strip(i, carry):
             at = pl.multiple_of(i * STRIP, STRIP)
@@ -151,49 +221,72 @@
             part[here, :] = total.astype(jnp.bfloat16)
             return carry
 
-        lax.fori_loop(0, m // STRIP, strip, 0)
-
-    def reduce_c(j):
-        g = flip(a, j)
+        lax.fori_loop(0, count // STRIP, strip, 0)
+
+    def reduce_c(p):
+        g, j = groups[p], slots[p]
         for bb in range(2):
             arrived(from_core.at[2 * j + bb], rcs.at[2 * j + bb], rcr.at[2 * j + bb])
-        add(g, 1 - b, from_core.at[2 * j + 1 - b])
-        send(
-            block(part, g, 1 - b, c), from_y.at[j], rys.at[j], ryr.at[j],
-            device(a, 1 - b, c),
-        )
-        add(g, b, from_core.at[2 * j + b])
-
-    def reduce_y(j):
-        g = flip(a, j)
-        arrived(from_y.at[j], rys.at[j], ryr.at[j])
-        add(g, b, from_y.at[j])
-        if j:
+        add(g, 1 - b, from_core.at[2 * j + 1 - b], 0, m)
+
+    def send_y(p):
+        g, j = groups[p], slots[p]
+        for h in range(HALVES):
+            k = HALVES * j + h
             send(
-                block(part, g, b, c), from_z.at[j], rzs.at[j], rzr.at[j],
-                device(g, b, c),
+                piece(part, g, 1 - b, c, h), from_y.at[j, pl.ds(h * half, half)],
+                rys.at[k], ryr.at[k], device(a, 1 - b, c),
             )
-
-    own = block(rows_all, a, b, c)
+        add(g, b, from_core.at[2 * j + b], 0, m)
+
+    def reduce_y(p):
+        g, j = groups[p], slots[p]
+        for h in range(HALVES):
+            k = HALVES * j + h
+            landed = from_y.at[j, pl.ds(h * half, half)]
+            arrived(landed, rys.at[k], ryr.at[k])
+            add(g, b, landed, h * half, half)
+            if p:
+                send(
+                    piece(part, g, b, c, h), from_z.at[j, pl.ds(h * half, half)],
+                    rzs.at[k], rzr.at[k], device(g, b, c),
+                )
+
+    gather_z(0)
+    gather_z(1)
+    gather_y(0)
+    gather_q(0)
+    gather_c(0)
+    compute(0)
+    gather_z(2)
+    reduce_c(0)
+    send_y(0)
+    gather_q(1)
+    gather_y(1)
+    for p in range(1, layers):
+        if p + 2 < layers:
+            gather_z(p + 2)
+        if p + 1 < layers:
+            gather_q(p + 1)
+        gather_c(p)
+        compute(p)
+        reduce_c(p)
+        if p != 1:
+            send_y(p)
+        if p == layers - 1:
+            send_y(1)
+        if p + 1 < layers:
+            gather_y(p + 1)
+        if p == 2:
+            reduce_y(0)
+        if p > 2:
+            reduce_y(p - 1)
+    reduce_y(layers - 1)
+    reduce_y(1)
     for j in range(1, layers):
-        send(own, own, zs.at[j], zr.at[j], device(flip(a, j), b, c))
-    gather_z(0)
-    gather_y(0)
-    if layers > 1:
-        gather_z(1)
-    for j in range(layers):
-        gather_c(j)
-        compute(j)
-        if j >= 1:
-            reduce_y(j - 1)
-        if j + 1 < layers:
-            gather_y(j + 1)
-        if j + 2 < layers:
-            gather_z(j + 2)
-        reduce_c(j)
-    reduce_y(layers - 1)
-    for j in range(1, layers):
-        arrived(from_z.at[j], rzs.at[j], rzr.at[j])
+        for h in range(HALVES):
+            k = HALVES * j + h
+            arrived(from_z.at[j, pl.ds(h * half, half)], rzs.at[k], rzr.at[k])
 
     def final(i, carry):
         at = pl.multiple_of(i * STRIP, STRIP)
@@ -208,6 +301,11 @@
     lax.fori_loop(0, m // STRIP, final, 0)
     for copy in sent:
         copy.wait_send()
+    for ready, copy in guarded:
+
+        @pl.when(ready)
+        def _(copy=copy):
+            copy.wait_send()
 
 
 def solution(mesh):
@@ -237,12 +335,13 @@
                 pltpu.VMEM((layers, m, d), bf),
                 pltpu.VMEM((layers, m, d), bf),
                 dma((2,)),
-                dma((layers,)), dma((layers,)),
+                dma((layers + 1,)), dma((layers,)),
+                dma((layers + 1,)), dma((layers,)),
                 dma((layers,)), dma((layers,)),
                 dma((2 * layers,)), dma((2 * layers,)),
                 dma((2 * layers,)), dma((2 * layers,)),
-                dma((layers,)), dma((layers,)),
-                dma((layers,)), dma((layers,)),
+                dma((HALVES * layers,)), dma((HALVES * layers,)),
+                dma((HALVES * layers,)), dma((HALVES * layers,)),
             ],
             compiler_params=pltpu.CompilerParams(
                 collective_id=0, has_side_effects=True, vmem_limit_bytes=67043328

time: 137 us -> 125 us (0.912); the launches traced: 137 us -> 124 us
  Pallas kernels: 135 us -> 122 us
    pallas_call x1, Pallas kernels: 135 us -> 122 us  [local(): pl.pallas_call(functools.partial(kernel, layers), out_shape=jax.ShapeDtyp...]
where the time goes in v2:
time: 125 us; the launch traced here: 124 us
  Pallas kernels  122 us (98%)
  local copies, waits for them, and re-layouts  1.87 us (1%)
    pallas_call x1, Pallas kernels, local(): pl.pallas_call(functools.partial(kernel, layers), out_shape=jax.ShapeDtyp...  122 us

profile of v2, /device:TPU:9, one launch (start us, length us, event | category | flops | bytes accessed | tf_op | source)
XLA Modules:
  0.0 123.5 jit_solution(10531148400048884457)
XLA Ops:
  0.0 121.7 %ffn.1 = bf16[64,4096]{1,0:T(8,128)(2,1)} custom-call(bf16[64,4096]{1,0:T(8,128)(2,1)} %nodes.1, f32[1,4096]{1,0:T(1,128)} %bitcast.3, bf16[4096,1024]{1,0:T(8,128)(2,1)} %w_in_hbm.1, f32[1,1024]{1,0:T(1,128)} %bitcast.5, bf16[1024,4096]{1,0:T(8,128)(2,1)} %w_out_hbm.1, f32[1,4096]{1,0:T(1,128)} %bitcast.4), custom_call_target="tpu_custom_call" | custom-call | flops 17179869184 | bytes 16777216 | tf_op jit(solution)/shard_map/ffn/pallas_call | solution.py:323
  121.7 1.9 %copy.8 = bf16[64,4096]{1,0:T(8,128)(2,1)} copy(bf16[64,4096]{1,0:T(8,128)(2,1)} %ffn.1) | data formatting | bytes 1048576
